TPU v7x, 32 devices: a whole 2x2x4 slice. The times are simulated.
32 devices in a mesh: row: 8 (over z, y), col: 4 (over x, core).
Axes of the slice: x: 2, y: 2, z: 4, core: 2. Of those that a mesh axis runs over, the one named last changes fastest.
Arguments:
- t2_amps: bfloat16 [2048, 1024], P('row', 'col'), may hold values from -6 to 6
- v_ints: bfloat16 [1024, 8192], P('row', 'col'), may hold values from -0.375 to 0.375
- t2_mask: int32 [16, 8], P('row', 'col'), may hold values from 0 to 1, as said below
- v_mask: int32 [8, 64], P('row', 'col'), may hold values from 0 to 1, as said below
Outputs:
- ladder: bfloat16 [2048, 8192], P('row', 'col')
Inputs may be any that keep to these rules, and one draw needn't show every extreme that they name: t2_mask[i, k] is 1 exactly where the symmetry sector of occupied-pair tile i equals that of contraction tile k, else 0; the sectors are 0 to 3, and each of the four labels at least one occupied-pair tile and at least one contraction tile. v_mask[k, n] is 1 exactly where the sector of contraction tile k (the same labels as in t2_mask) equals that of column tile n, else 0; the column tiles fall into aligned blocks of 16, one block for each col index, and in every block one sector labels exactly 8 tiles and no sector labels more than 8.
All inputs are finite; a program needn't handle non-finite values.
Results may differ from a plain program's by a relative error of at most 0.001.
Values may be sent and summed in bfloat16 or wider, within the bound.
A program may use at most 64 MiB of HBM per device.

v0:
```python
import jax
import jax.numpy as jnp
from jax import lax
from jax.sharding import PartitionSpec as P


def expand_mask(mask, tile):
    wide = jnp.repeat(jnp.repeat(mask, tile, axis=0), tile, axis=1)
    return wide.astype(jnp.bfloat16)


def on_device(t2_amps, v_ints, t2_mask, v_mask):
    tile = t2_amps.shape[0] // t2_mask.shape[0]
    t2_sparse = t2_amps * expand_mask(t2_mask, tile)
    v_sparse = v_ints * expand_mask(v_mask, tile)
    t2_whole = lax.all_gather(t2_sparse, "col", axis=1, tiled=True)
    ladder = jnp.dot(
        t2_whole,
        lax.all_gather(v_sparse, "row", axis=0, tiled=True),
        preferred_element_type=jnp.float32,
    )
    return ladder.astype(jnp.bfloat16)


def solution(mesh):
    return jax.shard_map(
        on_device,
        mesh=mesh,
        in_specs=(P("row", "col"), P("row", "col"), P("row", "col"), P("row", "col")),
        out_specs=P("row", "col"),
        check_vma=False,
    )
```

profile of v0, /device:TPU:0, one launch (start us, length us, event | category | flops | bytes accessed | tf_op | source)
XLA Modules:
  0.0 96.3 jit_solution(14550233758897805036)
XLA Ops:
  6.5 0.0 all-gather.2.cloned.1.call-start
  6.5 0.7 convert_bitcast_fusion
  7.2 0.1 broadcast_bitcast_fusion
  7.3 1.9 %broadcast_multiply_fusion = bf16[128,2048]{1,0:T(8,128)(2,1)} fusion(bf16[128,2048]{1,0:T(8,128)(2,1)} %param.5, bf16[2048]{0:T(1024)(128)(2,1)S(1)} %broadcast_bitcast_fusion), kind=kLoop, calls=%fused_computation.1 | loop fusion | flops 262144 | bytes 1052672 | tf_op jit(solution)/shard_map/mul | solution.py:15
  9.1 0.0 all-gather.2.cloned.1.call-update
  9.2 0.7 convert_element_type.25
  9.9 0.3 broadcast_in_dim.13
  10.2 0.9 bitcast_multiply_fusion
  11.1 8.6 %all_gather.6 = bf16[256,1024]{1,0:T(8,128)(2,1)S(1)} all-gather(bf16[256,256]{1,0:T(8,128)(2,1)S(1)} %bitcast_multiply_fusion), channel_id=1, replica_groups=mesh['row'=8,'col'=4] {'col'}, dimensions={1}, use_global_device_ids=true | all-gather | bytes 655360 | tf_op jit(solution)/shard_map/all_gather | solution.py:16
  19.8 65.2 %all-gather.2.cloned.1.call-done = bf16[1024,2048]{1,0:T(8,128)(2,1)} async-done(((bf16[128,2048]{1,0:T(8,128)(2,1)}), bf16[1024,2048]{1,0:T(8,128)(2,1)}) %all-gather.2.cloned.1.call-update) | async-done | bytes 4194320 | tf_op jit(solution)/shard_map/all_gather | solution.py:19
  85.0 4.4 %convolution_convert_fusion = bf16[256,2048]{1,0:T(8,128)(2,1)} fusion(bf16[256,1024]{1,0:T(8,128)(2,1)S(1)} %all_gather.6, bf16[1024,2048]{1,0:T(8,128)(2,1)} %all-gather.2.cloned.1.call-done), kind=kOutput, calls=%fused_computation | convolution fusion | flops 1074266112 | bytes 5767168 | tf_op jit(solution)/shard_map/dot_general | solution.py:17
  (1 shorter events, 0.0 us)
Async XLA Ops:
  6.5 78.5 %all-gather.2.cloned.1.call-start = ((), (), s32[]{:S(2)}) async-start(), calls=%async_computation | async-start | bytes 4718592 | tf_op jit(solution)/shard_map/all_gather | solution.py:19
Sparse Core Ops, SparseCore 0:
  9.5 75.5 all-gather.1
where the time goes:
time: 96.5 us; the launch traced here: 96.3 us
  waiting for transfers between devices  65.2 us (68%)
  between operations  13.4 us (14%)
  blocking collectives  8.65 us (9%)
  matrix products  4.41 us (5%)
  other arithmetic  4.15 us (4%)
    all_gather x1, waiting for transfers between devices, on_device(): lax.all_gather(v_sparse, 'row', axis=0, tiled=True)  65.2 us
    all_gather x1, blocking collectives, on_device(): t2_whole = lax.all_gather(t2_sparse, 'col', axis=1, tiled=True)  8.65 us
    dot_general x1, matrix products, on_device(): jnp.dot(t2_whole, lax.all_gather(v_sparse, 'row', axis=0, tiled=True), pr...  4.41 us
  transfers between devices with their start and end apart: 1, of which 1 were waited for; matrix products, arithmetic and copies ran while one was open for 2% of the time, Pallas kernels for 0%

commit v1 on v0

v1 whole, which is shorter than its diff:
```python
import functools

import jax
import jax.numpy as jnp
from jax import lax
from jax.experimental import pallas as pl
from jax.experimental.pallas import tpu as pltpu
from jax.sharding import PartitionSpec as P

MESH = pl.DeviceIdType.MESH


def grid_of(mesh):
    rows = mesh.shape["row"]
    ny = 1
    while 2 * (2 * ny) * (2 * ny) <= rows:
        ny *= 2
    return (rows // ny, ny) if rows % ny == 0 else (rows, 1)


def signs(d):
    return (0,) if d == 0 else (d, -d)


def gather_kernel(nz, ny, nc, tm_ref, vm_ref, t_ref, v_ref, o_ref, p_ref,
                  tbuf, vbuf, posbuf, acc, t_send, t_recv, send, recv):
    me, col = lax.axis_index("row"), lax.axis_index("col")
    z, y = me // ny, me % ny
    mr, kpc = tm_ref.shape
    nt = vm_ref.shape[1]
    tile = v_ref.shape[0]
    rows = t_ref.shape[0]
    cap = nt // 2
    nr = nz * ny
    f32 = jnp.float32

    dirs = ((1, 0), (-1, 0), (0, 1), (0, -1))

    def inside(dz, dy):
        ok = jnp.bool_(True)
        if dz > 0:
            ok = ok & (z + dz < nz)
        if dz < 0:
            ok = ok & (z + dz >= 0)
        if dy > 0:
            ok = ok & (y + dy < ny)
        if dy < 0:
            ok = ok & (y + dy >= 0)
        return ok

    live = [d for d in range(4) if (nz > 1 if d < 2 else ny > 1)]

    barrier = pltpu.get_barrier_semaphore()
    expect = jnp.int32(nc - 1)
    for d in live:
        dz, dy = dirs[d]
        ok = inside(dz, dy)
        expect = expect + ok.astype(jnp.int32)

        @pl.when(ok)
        def _():
            pl.semaphore_signal(barrier, inc=1, device_id=(me + dz * ny + dy, col), device_id_type=MESH)

    for s in range(1, nc):
        pl.semaphore_signal(barrier, inc=1, device_id=(me, lax.rem(col + s, nc)), device_id_type=MESH)

    bf16 = jnp.bfloat16
    count, slots = jnp.int32(0), []
    for n in range(nt):
        m = vm_ref[0, n]
        slots.append(jnp.broadcast_to((m * (count + 1)).astype(f32), (16, tile)))
        count = count + m

    def down(x):
        return jnp.broadcast_to(x.astype(bf16)[None], (tile // 16, 16, tile)).reshape(tile, tile)

    for j in range(cap):
        total = None
        for n in range(j, nt):
            hit = down(jnp.maximum(1.0 - jnp.abs(slots[n] - (j + 1.0)), 0.0))
            term = v_ref[:, n * tile:(n + 1) * tile] * hit
            total = term if total is None else total + term
        vbuf[me, :, j * tile:(j + 1) * tile] = total
    lane = lax.broadcasted_iota(jnp.int32, posbuf.shape[1:], 1)
    place = jnp.zeros(posbuf.shape[1:], f32)
    for n in range(nt):
        place = jnp.where(lane == n, slots[n][:8], place)
    posbuf[me] = place
    for i in range(mr):
        for k in range(kpc):
            part = t_ref[i * tile:(i + 1) * tile, k * tile:(k + 1) * tile]
            flag = down(jnp.broadcast_to(tm_ref[i, k].astype(f32), (16, tile)))
            tbuf[col, i * tile:(i + 1) * tile, k * tile:(k + 1) * tile] = part * flag
    row16 = lax.broadcasted_iota(jnp.int32, (tbuf.shape[1] - rows, tile), 0)
    for k in range(kpc):
        flags = jnp.zeros(row16.shape, f32)
        for i in range(mr):
            flags = jnp.where(row16 == i, tm_ref[i, k].astype(f32), flags)
        tbuf[col, rows:, k * tile:(k + 1) * tile] = flags.astype(tbuf.dtype)

    pl.semaphore_wait(barrier, expect)

    head = tile // 8
    cuts = [(0, head), (head, 3 * head), (4 * head, 2 * head), (6 * head, 2 * head)]
    small = len(cuts)

    def piece(src, c):
        if c == small:
            return posbuf.at[src]
        return vbuf.at[src, pl.ds(cuts[c][0], cuts[c][1])]

    def copy(src, c, d):
        dz, dy = dirs[d]
        return pltpu.make_async_remote_copy(
            src_ref=piece(src, c), dst_ref=piece(src, c),
            send_sem=send.at[d, src, c], recv_sem=recv.at[src, c],
            device_id=(me + dz * ny + dy, col), device_id_type=MESH)

    sent = []

    def forward(src, c, d, valid):
        dz, dy = dirs[d]
        ok = inside(dz, dy) if valid is None else valid & inside(dz, dy)

        @pl.when(ok)
        def _():
            copy(src, c, d).start()

        sent.append((src, c, d, ok))

    def arrive(src, c):
        pltpu.make_async_remote_copy(
            src_ref=piece(src, c), dst_ref=piece(src, c),
            send_sem=send.at[0, src, c], recv_sem=recv.at[src, c],
            device_id=(me, col), device_id_type=MESH).wait_recv()

    def step_dirs(a, b, first):
        zdir = [0] if a > 0 else [1] if a < 0 else [0, 1]
        ydir = [2] if b > 0 else [3] if b < 0 else [2, 3]
        if first:
            out = zdir + (ydir if a == 0 else [])
        else:
            out = (zdir if b == 0 else []) + ydir
        keep = []
        for d in out:
            if d not in live:
                continue
            if d < 2 and abs(a + dirs[d][0]) >= nz:
                continue
            if d >= 2 and abs(b + dirs[d][1]) >= ny:
                continue
            keep.append(d)
        return keep

    heads = [0, small]
    bodies = list(range(1, small))

    for c in [0, small] + bodies:
        for d in live:
            forward(me, c, d, None)

    t_copies = []
    for s in range(1, nc):
        t_copies.append(pltpu.make_async_remote_copy(
            src_ref=tbuf.at[col], dst_ref=tbuf.at[col],
            send_sem=t_send.at[s], recv_sem=t_recv.at[s],
            device_id=(me, lax.rem(col + s, nc)), device_id_type=MESH))
        t_copies[-1].start()

    def event(a, b, cs, first):
        valid = inside(-a, -b)
        src = me - a * ny - b
        for c in cs:
            @pl.when(valid)
            def _():
                arrive(src, c)

            for d in step_dirs(a, b, first):
                forward(src, c, d, valid)

    for key in range(1, nz + ny - 1):
        for db in range(min(key, ny - 1), -1, -1):
            da = key - db
            if da >= nz:
                continue
            for a in signs(da):
                for b in signs(db):
                    event(a, b, heads, True)
        for db in range(0, ny - 1):
            da = key - db
            if da >= nz or da < 0:
                continue
            for c in bodies:
                for a in signs(da):
                    for b in signs(db):
                        event(a, b, [c], False)

    for t in t_copies:
        t.wait()

    acc[...] = jnp.zeros_like(acc)
    wide = 2 * tile

    def multiply(src):
        left = tbuf[src // kpc, :rows, pl.ds(pl.multiple_of(lax.rem(src, kpc) * tile, tile), tile)]
        for n in range(0, cap * tile, wide):
            acc[:, n:n + wide] += jnp.dot(left, vbuf[src, :, n:n + wide], preferred_element_type=f32)

    def local(zz, carry):
        for yy in range(ny):
            pass
        multiply(zz * ny + y)
        return carry

    lax.fori_loop(0, nz, local, 0)

    for src, c, d, ok in sent[:len(sent) // 2]:
        @pl.when(ok)
        def _():
            copy(src, c, d).wait_send()

    far = [b for b in range(-(ny - 1), ny) if b != 0]

    def across(s, carry):
        dist = (s + 1) // 2
        a = jnp.where(s % 2 == 1, dist, -dist)
        zz = z - a
        for b in far:
            ok = (zz >= 0) & (zz < nz) & (y - b >= 0) & (y - b < ny)
            src = zz * ny + y - b

            @pl.when(ok)
            def _():
                if abs(b) == ny - 1:
                    for c in bodies:
                        arrive(src, c)
                multiply(src)
        return carry

    lax.fori_loop(0, 2 * nz - 1, across, 0)

    for src, c, d, ok in sent[len(sent) // 2:]:
        @pl.when(ok)
        def _():
            copy(src, c, d).wait_send()

    o_ref[...] = acc[...].astype(o_ref.dtype)

    p_ref[...] = jnp.zeros_like(p_ref)
    for i in range(mr):
        best = jnp.zeros((1, posbuf.shape[2]), f32)
        for src in range(nr):
            kk = (src % kpc) * tile
            flag = tbuf[src // kpc, rows:, kk:kk + tile].astype(f32)[i:i + 1]
            best = jnp.maximum(best, flag * posbuf[src, 0:1, :])
        p_ref[i:i + 1, :] = best.astype(jnp.int32)


def spread_kernel(per, p_ref, o_ref, out_ref):
    tile = out_ref.shape[1] // per
    for i in range(out_ref.shape[0] // tile):
        here = slice(i * tile, (i + 1) * tile)
        for q in range(per):
            slot = p_ref[i, pl.program_id(0) * per + q]
            at = pl.multiple_of(jnp.maximum(slot - 1, 0) * tile, tile)
            got = o_ref[here, pl.ds(at, tile)]
            out_ref[here, q * tile:(q + 1) * tile] = jnp.where(slot > 0, got, jnp.zeros_like(got))


def solution(mesh):
    nz, ny = grid_of(mesh)
    nc = mesh.shape["col"]

    def on_device(t2_amps, v_ints, t2_mask, v_mask):
        rows, kcols = t2_amps.shape
        tile, ncols = v_ints.shape
        mr = t2_mask.shape[0]
        nt = v_mask.shape[1]
        cap = nt // 2
        nr = nz * ny
        pieces = 5
        vmem = pl.BlockSpec(memory_space=pltpu.VMEM)
        smem = pl.BlockSpec(memory_space=pltpu.SMEM)
        dense, places = pl.pallas_call(
            functools.partial(gather_kernel, nz, ny, nc),
            name="gather",
            out_shape=(jax.ShapeDtypeStruct((rows, cap * tile), jnp.bfloat16),
                       jax.ShapeDtypeStruct((8, 128), jnp.int32)),
            in_specs=[smem, smem, vmem, vmem],
            out_specs=(vmem, vmem),
            scratch_shapes=[
                pltpu.VMEM((nc, rows + 16, kcols), jnp.bfloat16),
                pltpu.VMEM((nr, tile, cap * tile), jnp.bfloat16),
                pltpu.VMEM((nr, 8, 128), jnp.float32),
                pltpu.VMEM((rows, cap * tile), jnp.float32),
                pltpu.SemaphoreType.DMA((nc,)),
                pltpu.SemaphoreType.DMA((nc,)),
                pltpu.SemaphoreType.DMA((4, nr, pieces)),
                pltpu.SemaphoreType.DMA((nr, pieces)),
            ],
            compiler_params=pltpu.CompilerParams(collective_id=0, has_side_effects=True),
        )(t2_mask, v_mask, t2_amps, v_ints)
        per = max(nt // 4, 1)
        return pl.pallas_call(
            functools.partial(spread_kernel, per),
            name="spread",
            grid=(nt // per,),
            out_shape=jax.ShapeDtypeStruct((rows, ncols), jnp.bfloat16),
            in_specs=[smem, pl.BlockSpec((rows, cap * tile), lambda n: (0, 0))],
            out_specs=pl.BlockSpec((rows, per * tile), lambda n: (0, n)),
        )(places, dense)

    return jax.shard_map(
        on_device,
        mesh=mesh,
        in_specs=(P("row", "col"), P("row", "col"), P("row", "col"), P("row", "col")),
        out_specs=P("row", "col"),
        check_vma=False,
    )
```

time: 96.5 us -> 35.7 us (0.37)
  waiting for transfers between devices: 65.2 us -> 0 us
  Pallas kernels: 0 us -> 35.5 us
  between operations: 13.4 us -> 0.01 us
  blocking collectives: 8.65 us -> 0 us
  matrix products: 4.41 us -> 0 us
  other arithmetic: 4.15 us -> 0 us
    all_gather x1 -> x0, waiting for transfers between devices: 65.2 us -> none  [on_device(): lax.all_gather(v_sparse, 'row', axis=0, tiled=True)]
    pallas_call x0 -> x2, Pallas kernels: none -> 35.5 us  [the longest x1 32.8 us: on_device(): pl.pallas_call(functools.partial(gather_kernel, nz, ny, nc), name='gather...]
    all_gather x1 -> x0, blocking collectives: 8.65 us -> none  [on_device(): t2_whole = lax.all_gather(t2_sparse, 'col', axis=1, tiled=True)]
    dot_general x1 -> x0, matrix products: 4.41 us -> none  [on_device(): jnp.dot(t2_whole, lax.all_gather(v_sparse, 'row', axis=0, tiled=True), pr...]
    mul x2 -> x0, other arithmetic: 2.8 us -> none  [the longest x1 1.88 us: on_device(): v_sparse = v_ints * expand_mask(v_mask, tile)]
    convert_element_type x2 -> x0, other arithmetic: 1.34 us -> none  [expand_mask(): return wide.astype(jnp.bfloat16)]
  transfers between devices with their start and end apart: 1 -> 0, of which waited for: 1 -> 0; matrix products, arithmetic and copies ran while one was open for 2% -> 0% of each run, Pallas kernels for 0% -> 0%
where the time goes in v1:
time: 35.7 us; the launch traced here: 35.5 us
  Pallas kernels  35.5 us (99%)
    pallas_call x1, Pallas kernels, on_device(): pl.pallas_call(functools.partial(gather_kernel, nz, ny, nc), name='gather...  32.8 us
    pallas_call x1, Pallas kernels, on_device(): pl.pallas_call(functools.partial(spread_kernel, per), name='spread', grid...  2.75 us

profile of v1, /device:TPU:0, one launch (start us, length us, event | category | flops | bytes accessed | tf_op | source)
XLA Modules:
  0.0 35.5 jit_solution(10833402281422319736)
XLA Ops:
  0.0 32.8 %gather.1 = (bf16[256,1024]{1,0:T(8,128)(2,1)}, s32[8,128]{1,0:T(8,128)}) custom-call(s32[2,2]{1,0:T(2,128)} %tm_ref.1, s32[1,16]{1,0:T(1,128)} %vm_ref.1, bf16[256,256]{1,0:T(8,128)(2,1)} %t_ref.1, bf16[128,2048]{1,0:T(8,128)(2,1)} %v_ref.1), custom_call_target="tpu_custom_call" | custom-call | tf_op jit(solution)/shard_map/gather/pallas_call | solution.py:284
  32.8 2.7 %spread.1 = bf16[256,2048]{1,0:T(8,128)(2,1)} custom-call(s32[8,128]{1,0:T(8,128)} %get-tuple-element.7.p_ref, bf16[256,1024]{1,0:T(8,128)(2,1)} %get-tuple-element.8.o_ref), custom_call_target="tpu_custom_call" | custom-call | tf_op jit(solution)/shard_map/spread/pallas_call | solution.py:304

commit v2 on v1

--- a/solution.py
+++ b/solution.py
@@ -22,8 +22,8 @@
     return (0,) if d == 0 else (d, -d)
 
 
-def gather_kernel(nz, ny, nc, tm_ref, vm_ref, t_ref, v_ref, o_ref, p_ref,
-                  tbuf, vbuf, posbuf, acc, t_send, t_recv, send, recv):
+def gather_kernel(nz, ny, nc, tm_ref, vm_ref, t_hbm, v_hbm, o_ref, p_ref,
+                  t_ref, v_ref, load, tbuf, vbuf, posbuf, acc, t_send, t_recv, send, recv):
     me, col = lax.axis_index("row"), lax.axis_index("col")
     z, y = me // ny, me % ny
     mr, kpc = tm_ref.shape
@@ -64,6 +64,10 @@
     for s in range(1, nc):
         pl.semaphore_signal(barrier, inc=1, device_id=(me, lax.rem(col + s, nc)), device_id_type=MESH)
 
+    loads = [pltpu.make_async_copy(v_hbm, v_ref, load.at[0]), pltpu.make_async_copy(t_hbm, t_ref, load.at[1])]
+    for one in loads:
+        one.start()
+
     bf16 = jnp.bfloat16
     count, slots = jnp.int32(0), []
     for n in range(nt):
@@ -74,6 +78,8 @@
     def down(x):
         return jnp.broadcast_to(x.astype(bf16)[None], (tile // 16, 16, tile)).reshape(tile, tile)
 
+    for one in loads:
+        one.wait()
     for j in range(cap):
         total = None
         for n in range(j, nt):
@@ -101,7 +107,7 @@
     pl.semaphore_wait(barrier, expect)
 
     head = tile // 8
-    cuts = [(0, head), (head, 3 * head), (4 * head, 2 * head), (6 * head, 2 * head)]
+    cuts = [(0, head), (head, 2 * head), (3 * head, 2 * head), (5 * head, 2 * head), (7 * head, head)]
     small = len(cuts)
 
     def piece(src, c):
@@ -155,9 +161,9 @@
     heads = [0, small]
     bodies = list(range(1, small))
 
-    for c in [0, small] + bodies:
+    for cy, cz in zip(heads + bodies, bodies + heads):
         for d in live:
-            forward(me, c, d, None)
+            forward(me, cz if d < 2 else cy, d, None)
 
     t_copies = []
     for s in range(1, nc):
@@ -179,13 +185,6 @@
                 forward(src, c, d, valid)
 
     for key in range(1, nz + ny - 1):
-        for db in range(min(key, ny - 1), -1, -1):
-            da = key - db
-            if da >= nz:
-                continue
-            for a in signs(da):
-                for b in signs(db):
-                    event(a, b, heads, True)
         for db in range(0, ny - 1):
             da = key - db
             if da >= nz or da < 0:
@@ -194,6 +193,13 @@
                 for a in signs(da):
                     for b in signs(db):
                         event(a, b, [c], False)
+        for db in range(min(key, ny - 1), -1, -1):
+            da = key - db
+            if da >= nz:
+                continue
+            for a in signs(da):
+                for b in signs(db):
+                    event(a, b, heads, True)
 
     for t in t_copies:
         t.wait()
@@ -207,44 +213,10 @@
             acc[:, n:n + wide] += jnp.dot(left, vbuf[src, :, n:n + wide], preferred_element_type=f32)
 
     def local(zz, carry):
-        for yy in range(ny):
-            pass
         multiply(zz * ny + y)
         return carry
 
     lax.fori_loop(0, nz, local, 0)
-
-    for src, c, d, ok in sent[:len(sent) // 2]:
-        @pl.when(ok)
-        def _():
-            copy(src, c, d).wait_send()
-
-    far = [b for b in range(-(ny - 1), ny) if b != 0]
-
-    def across(s, carry):
-        dist = (s + 1) // 2
-        a = jnp.where(s % 2 == 1, dist, -dist)
-        zz = z - a
-        for b in far:
-            ok = (zz >= 0) & (zz < nz) & (y - b >= 0) & (y - b < ny)
-            src = zz * ny + y - b
-
-            @pl.when(ok)
-            def _():
-                if abs(b) == ny - 1:
-                    for c in bodies:
-                        arrive(src, c)
-                multiply(src)
-        return carry
-
-    lax.fori_loop(0, 2 * nz - 1, across, 0)
-
-    for src, c, d, ok in sent[len(sent) // 2:]:
-        @pl.when(ok)
-        def _():
-            copy(src, c, d).wait_send()
-
-    o_ref[...] = acc[...].astype(o_ref.dtype)
 
     p_ref[...] = jnp.zeros_like(p_ref)
     for i in range(mr):
@@ -255,9 +227,48 @@
             best = jnp.maximum(best, flag * posbuf[src, 0:1, :])
         p_ref[i:i + 1, :] = best.astype(jnp.int32)
 
-
-def spread_kernel(per, p_ref, o_ref, out_ref):
+    for src, c, d, ok in sent[:3 * len(sent) // 4]:
+        @pl.when(ok)
+        def _():
+            copy(src, c, d).wait_send()
+
+    far = [b for b in range(-(ny - 1), ny) if b != 0]
+
+    def across(s, carry):
+        dist = (s + 1) // 2
+        a = jnp.where(s % 2 == 1, dist, -dist)
+        zz = z - a
+        for b in far:
+            ok = (zz >= 0) & (zz < nz) & (y - b >= 0) & (y - b < ny)
+            src = zz * ny + y - b
+
+            @pl.when(ok)
+            def _():
+                if abs(b) == ny - 1:
+                    for c in bodies:
+                        arrive(src, c)
+                multiply(src)
+        return carry
+
+    lax.fori_loop(0, 2 * nz - 1, across, 0)
+
+    for src, c, d, ok in sent[3 * len(sent) // 4:]:
+        @pl.when(ok)
+        def _():
+            copy(src, c, d).wait_send()
+
+    o_ref[...] = acc[...].astype(o_ref.dtype)
+
+
+def spread_kernel(per, p_vec, o_ref, out_ref, p_ref, sem):
     tile = out_ref.shape[1] // per
+
+    @pl.when(pl.program_id(0) == 0)
+    def _():
+        one = pltpu.make_async_copy(p_vec, p_ref, sem)
+        one.start()
+        one.wait()
+
     for i in range(out_ref.shape[0] // tile):
         here = slice(i * tile, (i + 1) * tile)
         for q in range(per):
@@ -278,17 +289,20 @@
         nt = v_mask.shape[1]
         cap = nt // 2
         nr = nz * ny
-        pieces = 5
+        pieces = 6
         vmem = pl.BlockSpec(memory_space=pltpu.VMEM)
+        whole = pl.BlockSpec(memory_space=pl.ANY)
         smem = pl.BlockSpec(memory_space=pltpu.SMEM)
         dense, places = pl.pallas_call(
             functools.partial(gather_kernel, nz, ny, nc),
             name="gather",
-            out_shape=(jax.ShapeDtypeStruct((rows, cap * tile), jnp.bfloat16),
-                       jax.ShapeDtypeStruct((8, 128), jnp.int32)),
-            in_specs=[smem, smem, vmem, vmem],
+            out_shape=(pltpu.VMEM((rows, cap * tile), jnp.bfloat16), pltpu.VMEM((8, 128), jnp.int32)),
+            in_specs=[smem, smem, whole, whole],
             out_specs=(vmem, vmem),
             scratch_shapes=[
+                pltpu.VMEM((rows, kcols), jnp.bfloat16),
+                pltpu.VMEM((tile, ncols), jnp.bfloat16),
+                pltpu.SemaphoreType.DMA((2,)),
                 pltpu.VMEM((nc, rows + 16, kcols), jnp.bfloat16),
                 pltpu.VMEM((nr, tile, cap * tile), jnp.bfloat16),
                 pltpu.VMEM((nr, 8, 128), jnp.float32),
@@ -300,14 +314,17 @@
             ],
             compiler_params=pltpu.CompilerParams(collective_id=0, has_side_effects=True),
         )(t2_mask, v_mask, t2_amps, v_ints)
+        dense = pltpu.with_memory_space_constraint(dense, pltpu.VMEM)
+        places = pltpu.with_memory_space_constraint(places, pltpu.VMEM)
         per = max(nt // 4, 1)
         return pl.pallas_call(
             functools.partial(spread_kernel, per),
             name="spread",
             grid=(nt // per,),
             out_shape=jax.ShapeDtypeStruct((rows, ncols), jnp.bfloat16),
-            in_specs=[smem, pl.BlockSpec((rows, cap * tile), lambda n: (0, 0))],
+            in_specs=[vmem, vmem],
             out_specs=pl.BlockSpec((rows, per * tile), lambda n: (0, n)),
+            scratch_shapes=[pltpu.SMEM((8, 128), jnp.int32), pltpu.SemaphoreType.DMA],
         )(places, dense)
 
     return jax.shard_map(

time: 35.7 us -> 33.3 us (0.933)
  Pallas kernels: 35.5 us -> 33.1 us
    pallas_call x1, Pallas kernels: 32.8 us -> 30.8 us  [on_device(): pl.pallas_call(functools.partial(gather_kernel, nz, ny, nc), name='gather...]
    pallas_call x1, Pallas kernels: 2.75 us -> 2.29 us  [on_device(): pl.pallas_call(functools.partial(spread_kernel, per), name='spread', grid...]
where the time goes in v2:
time: 33.3 us; the launch traced here: 33.1 us
  Pallas kernels  33.1 us (99%)
    pallas_call x1, Pallas kernels, on_device(): pl.pallas_call(functools.partial(gather_kernel, nz, ny, nc), name='gather...  30.8 us
    pallas_call x1, Pallas kernels, on_device(): pl.pallas_call(functools.partial(spread_kernel, per), name='spread', grid...  2.29 us

profile of v2, /device:TPU:0, one launch (start us, length us, event | category | flops | bytes accessed | tf_op | source)
XLA Modules:
  0.0 33.1 jit_solution(17595938817897145951)
XLA Ops:
  0.0 30.8 %gather.1 = (bf16[256,1024]{1,0:T(8,128)(2,1)S(1)}, s32[8,128]{1,0:T(8,128)S(1)}) custom-call(s32[2,2]{1,0:T(2,128)} %tm_ref.1, s32[1,16]{1,0:T(1,128)} %vm_ref.1, bf16[256,256]{1,0:T(8,128)(2,1)} %t_hbm.1, bf16[128,2048]{1,0:T(8,128)(2,1)} %v_hbm.1), custom_call_target="tpu_custom_call" | custom-call | tf_op jit(solution)/shard_map/gather/pallas_call | solution.py:296
  30.8 2.3 %spread.1 = bf16[256,2048]{1,0:T(8,128)(2,1)} custom-call(s32[8,128]{1,0:T(8,128)S(1)} %get-tuple-element.7.p_vec, bf16[256,1024]{1,0:T(8,128)(2,1)S(1)} %get-tuple-element.8.o_ref), custom_call_target="tpu_custom_call" | custom-call | tf_op jit(solution)/shard_map/spread/pallas_call | solution.py:320

commit v3 on v2

--- a/solution.py
+++ b/solution.py
@@ -22,8 +22,8 @@
     return (0,) if d == 0 else (d, -d)
 
 
-def gather_kernel(nz, ny, nc, tm_ref, vm_ref, t_hbm, v_hbm, o_ref, p_ref,
-                  t_ref, v_ref, load, tbuf, vbuf, posbuf, acc, t_send, t_recv, send, recv):
+def gather_kernel(nz, ny, nc, tm_hbm, vm_hbm, t_hbm, v_hbm, o_ref, p_ref,
+                  tm_ref, vm_ref, t_ref, v_ref, p_vec, load, tbuf, vbuf, posbuf, acc, t_send, t_recv, send, recv):
     me, col = lax.axis_index("row"), lax.axis_index("col")
     z, y = me // ny, me % ny
     mr, kpc = tm_ref.shape
@@ -64,9 +64,12 @@
     for s in range(1, nc):
         pl.semaphore_signal(barrier, inc=1, device_id=(me, lax.rem(col + s, nc)), device_id_type=MESH)
 
-    loads = [pltpu.make_async_copy(v_hbm, v_ref, load.at[0]), pltpu.make_async_copy(t_hbm, t_ref, load.at[1])]
+    loads = [pltpu.make_async_copy(src, dst, load.at[i]) for i, (src, dst) in enumerate(
+        ((vm_hbm, vm_ref), (tm_hbm, tm_ref), (v_hbm, v_ref), (t_hbm, t_ref)))]
     for one in loads:
         one.start()
+    for one in loads[:2]:
+        one.wait()
 
     bf16 = jnp.bfloat16
     count, slots = jnp.int32(0), []
@@ -78,7 +81,7 @@
     def down(x):
         return jnp.broadcast_to(x.astype(bf16)[None], (tile // 16, 16, tile)).reshape(tile, tile)
 
-    for one in loads:
+    for one in loads[2:]:
         one.wait()
     for j in range(cap):
         total = None
@@ -107,13 +110,15 @@
     pl.semaphore_wait(barrier, expect)
 
     head = tile // 8
-    cuts = [(0, head), (head, 2 * head), (3 * head, 2 * head), (5 * head, 2 * head), (7 * head, head)]
+    full = cap * tile
+    cuts = [(0, head, 0, full), (head, 2 * head, 0, full), (3 * head, 2 * head, 0, full),
+            (5 * head, 2 * head, 0, full), (7 * head, head, 0, full)]
     small = len(cuts)
 
     def piece(src, c):
         if c == small:
             return posbuf.at[src]
-        return vbuf.at[src, pl.ds(cuts[c][0], cuts[c][1])]
+        return vbuf.at[src, pl.ds(cuts[c][0], cuts[c][1]), pl.ds(cuts[c][2], cuts[c][3])]
 
     def copy(src, c, d):
         dz, dy = dirs[d]
@@ -218,14 +223,17 @@
 
     lax.fori_loop(0, nz, local, 0)
 
-    p_ref[...] = jnp.zeros_like(p_ref)
+    p_vec[...] = jnp.zeros_like(p_vec)
     for i in range(mr):
         best = jnp.zeros((1, posbuf.shape[2]), f32)
         for src in range(nr):
             kk = (src % kpc) * tile
             flag = tbuf[src // kpc, rows:, kk:kk + tile].astype(f32)[i:i + 1]
             best = jnp.maximum(best, flag * posbuf[src, 0:1, :])
-        p_ref[i:i + 1, :] = best.astype(jnp.int32)
+        p_vec[i:i + 1, :] = best.astype(jnp.int32)
+
+    give = pltpu.make_async_copy(p_vec, p_ref, load.at[4])
+    give.start()
 
     for src, c, d, ok in sent[:3 * len(sent) // 4]:
         @pl.when(ok)
@@ -257,17 +265,12 @@
         def _():
             copy(src, c, d).wait_send()
 
+    give.wait()
     o_ref[...] = acc[...].astype(o_ref.dtype)
 
 
-def spread_kernel(per, p_vec, o_ref, out_ref, p_ref, sem):
+def spread_kernel(per, p_ref, o_ref, out_ref):
     tile = out_ref.shape[1] // per
-
-    @pl.when(pl.program_id(0) == 0)
-    def _():
-        one = pltpu.make_async_copy(p_vec, p_ref, sem)
-        one.start()
-        one.wait()
 
     for i in range(out_ref.shape[0] // tile):
         here = slice(i * tile, (i + 1) * tile)
@@ -296,13 +299,16 @@
         dense, places = pl.pallas_call(
             functools.partial(gather_kernel, nz, ny, nc),
             name="gather",
-            out_shape=(pltpu.VMEM((rows, cap * tile), jnp.bfloat16), pltpu.VMEM((8, 128), jnp.int32)),
-            in_specs=[smem, smem, whole, whole],
-            out_specs=(vmem, vmem),
+            out_shape=(pltpu.VMEM((rows, cap * tile), jnp.bfloat16), pltpu.SMEM((8, 128), jnp.int32)),
+            in_specs=[whole] * 4,
+            out_specs=(vmem, smem),
             scratch_shapes=[
+                pltpu.SMEM(t2_mask.shape, jnp.int32),
+                pltpu.SMEM(v_mask.shape, jnp.int32),
                 pltpu.VMEM((rows, kcols), jnp.bfloat16),
                 pltpu.VMEM((tile, ncols), jnp.bfloat16),
-                pltpu.SemaphoreType.DMA((2,)),
+                pltpu.VMEM((8, 128), jnp.int32),
+                pltpu.SemaphoreType.DMA((5,)),
                 pltpu.VMEM((nc, rows + 16, kcols), jnp.bfloat16),
                 pltpu.VMEM((nr, tile, cap * tile), jnp.bfloat16),
                 pltpu.VMEM((nr, 8, 128), jnp.float32),
@@ -315,16 +321,15 @@
             compiler_params=pltpu.CompilerParams(collective_id=0, has_side_effects=True),
         )(t2_mask, v_mask, t2_amps, v_ints)
         dense = pltpu.with_memory_space_constraint(dense, pltpu.VMEM)
-        places = pltpu.with_memory_space_constraint(places, pltpu.VMEM)
+        places = pltpu.with_memory_space_constraint(places, pltpu.SMEM)
         per = max(nt // 4, 1)
         return pl.pallas_call(
             functools.partial(spread_kernel, per),
             name="spread",
             grid=(nt // per,),
             out_shape=jax.ShapeDtypeStruct((rows, ncols), jnp.bfloat16),
-            in_specs=[vmem, vmem],
+            in_specs=[smem, vmem],
             out_specs=pl.BlockSpec((rows, per * tile), lambda n: (0, n)),
-            scratch_shapes=[pltpu.SMEM((8, 128), jnp.int32), pltpu.SemaphoreType.DMA],
         )(places, dense)
 
     return jax.shard_map(

time: 33.3 us -> 31.9 us (0.958)
  Pallas kernels: 33.1 us -> 31.8 us
    pallas_call x1, Pallas kernels: 30.8 us -> 30.1 us  [on_device(): pl.pallas_call(functools.partial(gather_kernel, nz, ny, nc), name='gather...]
    pallas_call x1, Pallas kernels: 2.29 us -> 1.67 us  [on_device(): pl.pallas_call(functools.partial(spread_kernel, per), name='spread', grid...]
where the time goes in v3:
time: 31.9 us; the launch traced here: 31.8 us
  Pallas kernels  31.8 us (100%)
    pallas_call x1, Pallas kernels, on_device(): pl.pallas_call(functools.partial(gather_kernel, nz, ny, nc), name='gather...  30.1 us
    pallas_call x1, Pallas kernels, on_device(): pl.pallas_call(functools.partial(spread_kernel, per), name='spread', grid...  1.67 us

profile of v3, /device:TPU:0, one launch (start us, length us, event | category | flops | bytes accessed | tf_op | source)
XLA Modules:
  0.0 31.8 jit_solution(14579468405318037669)
XLA Ops:
  0.0 30.1 %gather.1 = (bf16[256,1024]{1,0:T(8,128)(2,1)S(1)}, s32[8,128]{1,0:T(8,128)S(4)}) custom-call(s32[2,2]{1,0:T(2,128)} %tm_hbm.1, s32[1,16]{1,0:T(1,128)} %vm_hbm.1, bf16[256,256]{1,0:T(8,128)(2,1)} %t_hbm.1, bf16[128,2048]{1,0:T(8,128)(2,1)} %v_hbm.1), custom_call_target="tpu_custom_call" | custom-call | tf_op jit(solution)/shard_map/gather/pallas_call | solution.py:299
  30.1 1.7 %spread.1 = bf16[256,2048]{1,0:T(8,128)(2,1)} custom-call(s32[8,128]{1,0:T(8,128)S(4)} %get-tuple-element.7.p_ref, bf16[256,1024]{1,0:T(8,128)(2,1)S(1)} %get-tuple-element.8.o_ref), custom_call_target="tpu_custom_call" | custom-call | tf_op jit(solution)/shard_map/spread/pallas_call | solution.py:326
